TPU v7x, 512 devices: a whole 4x8x8 slice. The times are simulated.
512 devices in a mesh: rows: 128 (over z, y, core), feat: 4 (over x).
Axes of the slice: x: 4, y: 8, z: 8, core: 2. Of those that a mesh axis runs over, the one named last changes fastest.
Arguments:
- codes: int32 [262144, 512], P('rows', 'feat'), may hold values from 0 to 31
- node_ids: int32 [262144], P('rows'), may hold values from 0 to 127
- bag: int32 [262144], P('rows'), may hold values from 0 to 3
- response: bfloat16 [262144], P('rows'), may hold values from -6 to 6
- owner_slot: int32 [128], replicated, may hold values from 0 to 127, each once
- chosen_feature: int32 [128], replicated, may hold values from 0 to 511
- chosen_bin: int32 [128], replicated, may hold values from 0 to 30
Outputs:
- gains: float32 [128, 16384], P('rows', 'feat')
- best_gain: float32 [128], P('rows')
- child_ids: int32 [262144], P('rows')
All inputs are finite; a program needn't handle non-finite values.
Results may differ from a plain program's by a relative error of at most 0.0003.
Values sent between devices are 32-bit elements; how exact they have to be, the bound alone decides.
A program may use at most 64 MiB of HBM per device.

v0:
```python
import jax
import jax.numpy as jnp
from jax import lax
from jax.sharding import Mesh
from jax.sharding import PartitionSpec as P

BINS = 32
ROWS = ("rows_0", "rows_1", "rows_2")


LAMBDA = 1.0


def in_blocks(shard, dim, length):
    before, after = (shard.shape[:dim], shard.shape[dim + 1 :])
    return jnp.moveaxis(shard.reshape(*before, length, -1, *after), dim, 0)


def sum_at_owner(shard, axis, dim):
    length = lax.axis_size(axis)
    tiles = lax.all_to_all(in_blocks(shard, dim, length), axis, 0, 0, tiled=True)
    return jnp.sum(tiles, axis=0)


def sum_in_two_steps(shard, axes, dim):
    far, near = axes
    tiles = in_blocks(shard, dim, lax.axis_size(far))
    nearer = sum_at_owner(tiles, near, dim + 1)
    arrived = lax.all_to_all(nearer, far, split_axis=0, concat_axis=0, tiled=True)
    return arrived.sum(axis=0)


def copy_for_each(shard, axis):
    copies = jnp.broadcast_to(shard, (lax.axis_size(axis), *shard.shape))
    return lax.all_to_all(copies, axis, split_axis=0, concat_axis=0, tiled=True)


def over_copies(shard, axis):
    everything = copy_for_each(shard, axis)
    return jnp.max(everything, axis=0)


def taken_together(shard, axis):
    return copy_for_each(shard, axis).sum(axis=0)


def per_device(codes, node_ids, bag, response, owner_slot, chosen_feature, chosen_bin):
    rows_dev, feat_dev = codes.shape
    nodes = owner_slot.shape[0]
    owned = nodes // lax.axis_size(ROWS)
    node_iota = jnp.arange(nodes, dtype=jnp.int32)
    match = node_ids[:, None] == node_iota[None, :]
    slot = jnp.sum(jnp.where(match, owner_slot[None, :], 0), axis=1)
    feat_row = jnp.sum(jnp.where(match, chosen_feature[None, :], 0), axis=1)
    bin_row = jnp.sum(jnp.where(match, chosen_bin[None, :], 0), axis=1)
    block = 256
    turns = rows_dev // block
    codes_blocks = codes.reshape(turns, block, feat_dev)
    slot_blocks = slot.reshape(turns, block)
    weight_blocks = bag.astype(jnp.bfloat16).reshape(turns, block)
    value_blocks = response.reshape(turns, block)
    bin_iota = jnp.arange(BINS, dtype=jnp.int32)
    count_iota = jnp.arange(nodes, dtype=jnp.int32)

    def step(total, items):
        code_part, slot_part, weight_part, value_part = items
        spread = (code_part[:, :, None] == bin_iota[None, None, :]).astype(jnp.bfloat16)
        spread = (spread * weight_part[:, None, None]).reshape(block, feat_dev * BINS)
        pick = (slot_part[:, None] - 0 == count_iota[None, :]).astype(jnp.bfloat16)
        scaled = pick * value_part[:, None]
        sum_w = jnp.einsum("rn,rk->nk", pick, spread, preferred_element_type=jnp.float32)
        sum_g = jnp.einsum("rn,rk->nk", scaled, spread, preferred_element_type=jnp.float32)
        return (total + jnp.concatenate([sum_w, sum_g], axis=1), None)

    empty = jnp.zeros((nodes, 2 * feat_dev * BINS), jnp.float32)
    total, _ = lax.scan(step, empty, (codes_blocks, slot_blocks, weight_blocks, value_blocks))
    hist = sum_in_two_steps(total, (("rows_0", "rows_1"), "rows_2"), 0)
    width = feat_dev * BINS
    hist_w = hist[:, :width].reshape(owned, feat_dev, BINS)
    hist_g = hist[:, width:].reshape(owned, feat_dev, BINS)
    left_w = jnp.cumsum(hist_w, axis=2)
    left_g = jnp.cumsum(hist_g, axis=2)
    total_w = jnp.sum(hist_w, axis=2, keepdims=True)
    total_g = jnp.sum(hist_g, axis=2, keepdims=True)
    right_w = total_w - left_w
    right_g = total_g - left_g
    gains = (
        left_g * left_g / (left_w + LAMBDA)
        + right_g * right_g / (right_w + LAMBDA)
        - total_g * total_g / (total_w + LAMBDA)
    )
    gains = gains.reshape(owned, width)
    best_gain = over_copies(jnp.max(gains, axis=1), "feat")
    local = feat_row - lax.axis_index("feat") * feat_dev
    inside = (local >= 0) & (local < feat_dev)
    local_iota = jnp.arange(feat_dev, dtype=jnp.int32)
    code = jnp.sum(jnp.where(local_iota[None, :] == local[:, None], codes, 0), axis=1)
    flag = jnp.where(inside & (code > bin_row), 1.0, 0.0).astype(jnp.float32)
    right = taken_together(flag, "feat") > 0.5
    child_ids = 2 * node_ids + right.astype(jnp.int32)
    return (gains, best_gain, child_ids)


def solution(mesh):
    split = Mesh(
        mesh.devices.reshape(8, 8, 2, mesh.shape["feat"]), ("rows_0", "rows_1", "rows_2", "feat")
    )
    placed = (P(ROWS, "feat"), P(ROWS), P(ROWS), P(ROWS), P(), P(), P())
    return jax.shard_map(
        per_device,
        mesh=split,
        in_specs=placed,
        out_specs=(P(ROWS, "feat"), P(ROWS), P(ROWS)),
        check_vma=False,
    )
```

profile of v0, /device:TPU:24, one launch (start us, length us, event | category | flops | bytes accessed | tf_op | source)
XLA Modules:
  0.0 189.9 jit_solution(4482034689749807699)
XLA Ops:
  2.0 2.0 %select_reduce_fusion = (s32[2048]{0:T(1024)S(1)}, s32[2048]{0:T(1024)S(1)}, s32[2048]{0:T(1024)S(1)}) fusion(s32[128]{0:T(128)} %param.15, s32[2048]{0:T(1024)} %param.10, s32[128]{0:T(128)} %param.14, s32[128]{0:T(128)} %param.13), kind=kLoop, calls=%fused_computation.19 | loop fusion | flops 1828864 | bytes 34304 | tf_op jit(solution)/shard_map/reduce_sum | solution.py:55
  4.1 66.7 %while.11 = (s32[]{:T(128)}, f32[128,8192]{1,0:T(8,128)}, s32[8,256]{1,0:T(8,128)S(1)}, s32[8,256,128]{2,1,0:T(8,128)}, bf16[8,256]{1,0:T(8,128)(2,1)S(1)}, /*in...) while((s32[]{:T(128)}, f32[128,8192]{1,0:T(8,128)}, s32[8,256]{1,0:T(8,128)S(1)}, ...), condition=%wide.region_2.3_spmd.clone, body=%wide.region_1.2_spmd.clone.sunk | while | flops 542244864 | bytes 57351336 | solution.py:76
  4.2 0.9 constant_dynamic-slice_fusion.4
  6.0 0.9 fusion.37
  6.9 0.9 fusion.38
  7.8 1.3 copy-done
  9.1 1.4 maximum_add_fusion.2
  10.5 2.0 %copy-done.1 = f32[128,8192]{1,0:T(8,128)} copy-done((f32[128,8192]{1,0:T(8,128)}, f32[128,8192]{1,0:T(8,128)S(1)}, u32[]{:S(2)}) %copy-start.1) | copy-done | bytes 4194328 | tf_op jit(solution)/shard_map/while
  12.6 0.9 constant_dynamic-slice_fusion.4
  13.6 0.7 fusion.36
  14.3 0.9 fusion.37
  15.3 0.9 fusion.38
  16.2 1.3 copy-done
  17.5 1.4 maximum_add_fusion.2
  18.8 2.0 %copy-done.1 = f32[128,8192]{1,0:T(8,128)} copy-done((f32[128,8192]{1,0:T(8,128)}, f32[128,8192]{1,0:T(8,128)S(1)}, u32[]{:S(2)}) %copy-start.1) | copy-done | bytes 4194328 | tf_op jit(solution)/shard_map/while
  20.9 0.9 constant_dynamic-slice_fusion.4
  22.7 0.9 fusion.37
  23.6 0.9 fusion.38
  24.5 1.3 copy-done
  25.8 1.4 maximum_add_fusion.2
  27.2 2.0 %copy-done.1 = f32[128,8192]{1,0:T(8,128)} copy-done((f32[128,8192]{1,0:T(8,128)}, f32[128,8192]{1,0:T(8,128)S(1)}, u32[]{:S(2)}) %copy-start.1) | copy-done | bytes 4194328 | tf_op jit(solution)/shard_map/while
  29.3 0.9 constant_dynamic-slice_fusion.4
  31.0 0.9 fusion.37
  32.0 0.9 fusion.38
  32.9 1.3 copy-done
  34.1 1.4 maximum_add_fusion.2
  35.5 2.0 %copy-done.1 = f32[128,8192]{1,0:T(8,128)} copy-done((f32[128,8192]{1,0:T(8,128)}, f32[128,8192]{1,0:T(8,128)S(1)}, u32[]{:S(2)}) %copy-start.1) | copy-done | bytes 4194328 | tf_op jit(solution)/shard_map/while
  37.6 0.9 constant_dynamic-slice_fusion.4
  39.3 0.9 fusion.37
  40.3 0.9 fusion.38
  41.2 1.3 copy-done
  42.5 1.4 maximum_add_fusion.2
  43.9 2.0 %copy-done.1 = f32[128,8192]{1,0:T(8,128)} copy-done((f32[128,8192]{1,0:T(8,128)}, f32[128,8192]{1,0:T(8,128)S(1)}, u32[]{:S(2)}) %copy-start.1) | copy-done | bytes 4194328 | tf_op jit(solution)/shard_map/while
  45.9 0.9 constant_dynamic-slice_fusion.4
  47.7 0.9 fusion.37
  48.6 0.9 fusion.38
  49.5 1.3 copy-done
  50.8 1.4 maximum_add_fusion.2
  52.2 2.0 %copy-done.1 = f32[128,8192]{1,0:T(8,128)} copy-done((f32[128,8192]{1,0:T(8,128)}, f32[128,8192]{1,0:T(8,128)S(1)}, u32[]{:S(2)}) %copy-start.1) | copy-done | bytes 4194328 | tf_op jit(solution)/shard_map/while
  54.3 0.9 constant_dynamic-slice_fusion.4
  56.0 0.9 fusion.37
  57.0 0.9 fusion.38
  57.9 1.3 copy-done
  59.1 1.4 maximum_add_fusion.2
  60.5 2.0 %copy-done.1 = f32[128,8192]{1,0:T(8,128)} copy-done((f32[128,8192]{1,0:T(8,128)}, f32[128,8192]{1,0:T(8,128)S(1)}, u32[]{:S(2)}) %copy-start.1) | copy-done | bytes 4194328 | tf_op jit(solution)/shard_map/while
  62.6 0.9 constant_dynamic-slice_fusion.4
  64.4 0.9 fusion.37
  65.3 0.9 fusion.38
  66.2 1.3 copy-done
  67.5 1.4 maximum_add_fusion.2
  68.9 2.0 %copy-done.1 = f32[128,8192]{1,0:T(8,128)} copy-done((f32[128,8192]{1,0:T(8,128)}, f32[128,8192]{1,0:T(8,128)S(1)}, u32[]{:S(2)}) %copy-start.1) | copy-done | bytes 4194328 | tf_op jit(solution)/shard_map/while
  70.8 5.8 %reshape_reshape.3 = f32[64,2,1,8192]{3,1,0,2:T(2,128)} reshape(f32[128,8192]{1,0:T(8,128)} %get-tuple-element.45) | data formatting | bytes 8388608 | tf_op jit(solution)/shard_map/reshape;reshape | solution.py:16
  76.7 6.6 %copy.37 = f32[2,64,1,8192]{3,1,2,0:T(8,128)} copy(f32[2,64,1,8192]{3,0,1,2:T(2,128)} %bitcast.56) | data formatting | bytes 8388608 | tf_op jit(solution)/shard_map/transpose | solution.py:16
  83.2 5.7 %all-to-all-start = ((f32[2,64,1,8192]{3,1,2,0:T(8,128)}), f32[2,64,1,8192]{3,1,2,0:T(8,128)}, u32[]{:S(2)}, u32[]{:S(2)}) async-start(f32[2,64,1,8192]{3,1,2,0:T(8,128)} %copy.37), calls=%async_computation | async-start | bytes 8388608 | tf_op jit(solution)/shard_map/all_to_all | solution.py:21
  89.7 3.8 %all-to-all-done = f32[2,64,1,8192]{3,1,2,0:T(8,128)} async-done(((f32[2,64,1,8192]{3,1,2,0:T(8,128)}), f32[2,64,1,8192]{3,1,2,0:T(8,128)}, u32[]{:S(2)}, u32[]{:S(2)}) %all-to-all-start) | async-done | bytes 4194336 | tf_op jit(solution)/shard_map/all_to_all | solution.py:21
  94.1 4.3 %all-to-all-start.3 = ((f32[4,1,2048]{2,1,0:T(1,128)}), f32[4,1,2048]{2,1,0:T(1,128)S(1)}, u32[]{:S(2)}, u32[]{:S(2)}) async-start(f32[4,1,2048]{2,1,0:T(1,128)} %broadcast_in_dim.66), calls=%async_computation.3 | async-start | bytes 65536 | tf_op jit(solution)/shard_map/all_to_all | solution.py:35
  98.4 2.7 %reduce_sum.86 = f32[64,8192]{1,0:T(8,128)S(1)} reduce(f32[2,64,1,8192]{3,1,2,0:T(8,128)} %all-to-all-done, f32[]{:T(128)} %constant.17.clone.1), dimensions={0,2}, to_apply=%region_3.4 | reduce | flops 524288 | bytes 6291460 | tf_op jit(solution)/shard_map/reduce_sum | solution.py:22
  101.1 3.7 %reduce_sum.87 = f32[64,1,8192]{2,1,0:T(1,128)} reshape(f32[64,8192]{1,0:T(8,128)S(1)} %reduce_sum.86) | data formatting | bytes 4194304 | tf_op jit(solution)/shard_map/reduce_sum | solution.py:22
  104.8 16.5 %all-to-all-start.1 = ((f32[64,1,8192]{2,1,0:T(1,128)}), f32[64,1,8192]{2,1,0:T(1,128)S(1)}, u32[]{:S(2)}, u32[]{:S(2)}) async-start(f32[64,1,8192]{2,1,0:T(1,128)} %reduce_sum.87), calls=%async_computation.1 | async-start | bytes 4194304 | tf_op jit(solution)/shard_map/all_to_all | solution.py:29
  121.9 52.0 %all-to-all-done.1 = f32[64,1,8192]{2,1,0:T(1,128)S(1)} async-done(((f32[64,1,8192]{2,1,0:T(1,128)}), f32[64,1,8192]{2,1,0:T(1,128)S(1)}, u32[]{:S(2)}, u32[]{:S(2)}) %all-to-all-start.1) | async-done | bytes 2097184 | tf_op jit(solution)/shard_map/all_to_all | solution.py:29
  173.9 1.8 reduce_sum.88
  177.3 1.2 broadcast_in_dim.61
  178.5 5.6 %all-to-all-start.2 = ((f32[4,1,1]{2,1,0:T(1,128)}), f32[4,1,1]{2,1,0:T(1,128)S(1)}, u32[]{:S(2)}, u32[]{:S(2)}) async-start(f32[4,1,1]{2,1,0:T(1,128)} %broadcast_in_dim.61), calls=%async_computation.2 | async-start | bytes 4096 | tf_op jit(solution)/shard_map/all_to_all | solution.py:35
  185.6 3.7 %all-to-all-done.2 = f32[4,1,1]{2,1,0:T(1,128)S(1)} async-done(((f32[4,1,1]{2,1,0:T(1,128)}), f32[4,1,1]{2,1,0:T(1,128)S(1)}, u32[]{:S(2)}, u32[]{:S(2)}) %all-to-all-start.2) | async-done | bytes 48 | tf_op jit(solution)/shard_map/all_to_all | solution.py:35
  (102 shorter events, 13.6 us)
Async XLA Ops:
  6.9 2.2 %copy-start = (f32[128,8192]{1,0:T(8,128)S(1)}, f32[128,8192]{1,0:T(8,128)}, u32[]{:S(2)}) copy-start(f32[128,8192]{1,0:T(8,128)} %get-tuple-element.170) | copy-start | bytes 12582916 | tf_op jit(solution)/shard_map/while
  10.5 2.0 %copy-start.1 = (f32[128,8192]{1,0:T(8,128)}, f32[128,8192]{1,0:T(8,128)S(1)}, u32[]{:S(2)}) copy-start(f32[128,8192]{1,0:T(8,128)S(1)} %maximum_add_fusion.2) | copy-start | bytes 12582916 | tf_op jit(solution)/shard_map/while
  15.3 2.2 %copy-start = (f32[128,8192]{1,0:T(8,128)S(1)}, f32[128,8192]{1,0:T(8,128)}, u32[]{:S(2)}) copy-start(f32[128,8192]{1,0:T(8,128)} %get-tuple-element.170) | copy-start | bytes 12582916 | tf_op jit(solution)/shard_map/while
  18.8 2.0 %copy-start.1 = (f32[128,8192]{1,0:T(8,128)}, f32[128,8192]{1,0:T(8,128)S(1)}, u32[]{:S(2)}) copy-start(f32[128,8192]{1,0:T(8,128)S(1)} %maximum_add_fusion.2) | copy-start | bytes 12582916 | tf_op jit(solution)/shard_map/while
  23.6 2.2 %copy-start = (f32[128,8192]{1,0:T(8,128)S(1)}, f32[128,8192]{1,0:T(8,128)}, u32[]{:S(2)}) copy-start(f32[128,8192]{1,0:T(8,128)} %get-tuple-element.170) | copy-start | bytes 12582916 | tf_op jit(solution)/shard_map/while
  27.2 2.0 %copy-start.1 = (f32[128,8192]{1,0:T(8,128)}, f32[128,8192]{1,0:T(8,128)S(1)}, u32[]{:S(2)}) copy-start(f32[128,8192]{1,0:T(8,128)S(1)} %maximum_add_fusion.2) | copy-start | bytes 12582916 | tf_op jit(solution)/shard_map/while
  31.9 2.2 %copy-start = (f32[128,8192]{1,0:T(8,128)S(1)}, f32[128,8192]{1,0:T(8,128)}, u32[]{:S(2)}) copy-start(f32[128,8192]{1,0:T(8,128)} %get-tuple-element.170) | copy-start | bytes 12582916 | tf_op jit(solution)/shard_map/while
  35.5 2.0 %copy-start.1 = (f32[128,8192]{1,0:T(8,128)}, f32[128,8192]{1,0:T(8,128)S(1)}, u32[]{:S(2)}) copy-start(f32[128,8192]{1,0:T(8,128)S(1)} %maximum_add_fusion.2) | copy-start | bytes 12582916 | tf_op jit(solution)/shard_map/while
  40.3 2.2 %copy-start = (f32[128,8192]{1,0:T(8,128)S(1)}, f32[128,8192]{1,0:T(8,128)}, u32[]{:S(2)}) copy-start(f32[128,8192]{1,0:T(8,128)} %get-tuple-element.170) | copy-start | bytes 12582916 | tf_op jit(solution)/shard_map/while
  43.8 2.0 %copy-start.1 = (f32[128,8192]{1,0:T(8,128)}, f32[128,8192]{1,0:T(8,128)S(1)}, u32[]{:S(2)}) copy-start(f32[128,8192]{1,0:T(8,128)S(1)} %maximum_add_fusion.2) | copy-start | bytes 12582916 | tf_op jit(solution)/shard_map/while
  48.6 2.2 %copy-start = (f32[128,8192]{1,0:T(8,128)S(1)}, f32[128,8192]{1,0:T(8,128)}, u32[]{:S(2)}) copy-start(f32[128,8192]{1,0:T(8,128)} %get-tuple-element.170) | copy-start | bytes 12582916 | tf_op jit(solution)/shard_map/while
  52.2 2.0 %copy-start.1 = (f32[128,8192]{1,0:T(8,128)}, f32[128,8192]{1,0:T(8,128)S(1)}, u32[]{:S(2)}) copy-start(f32[128,8192]{1,0:T(8,128)S(1)} %maximum_add_fusion.2) | copy-start | bytes 12582916 | tf_op jit(solution)/shard_map/while
  57.0 2.2 %copy-start = (f32[128,8192]{1,0:T(8,128)S(1)}, f32[128,8192]{1,0:T(8,128)}, u32[]{:S(2)}) copy-start(f32[128,8192]{1,0:T(8,128)} %get-tuple-element.170) | copy-start | bytes 12582916 | tf_op jit(solution)/shard_map/while
  60.5 2.0 %copy-start.1 = (f32[128,8192]{1,0:T(8,128)}, f32[128,8192]{1,0:T(8,128)S(1)}, u32[]{:S(2)}) copy-start(f32[128,8192]{1,0:T(8,128)S(1)} %maximum_add_fusion.2) | copy-start | bytes 12582916 | tf_op jit(solution)/shard_map/while
  65.3 2.2 %copy-start = (f32[128,8192]{1,0:T(8,128)S(1)}, f32[128,8192]{1,0:T(8,128)}, u32[]{:S(2)}) copy-start(f32[128,8192]{1,0:T(8,128)} %get-tuple-element.170) | copy-start | bytes 12582916 | tf_op jit(solution)/shard_map/while
  68.9 2.0 %copy-start.1 = (f32[128,8192]{1,0:T(8,128)}, f32[128,8192]{1,0:T(8,128)S(1)}, u32[]{:S(2)}) copy-start(f32[128,8192]{1,0:T(8,128)S(1)} %maximum_add_fusion.2) | copy-start | bytes 12582916 | tf_op jit(solution)/shard_map/while
  83.2 5.8 %copy-start.2 = (s32[8,256,128]{2,1,0:T(8,128)S(1)}, s32[8,256,128]{2,1,0:T(8,128)}, u32[]{:S(2)}) copy-start(s32[8,256,128]{2,1,0:T(8,128)} %get-tuple-element.190) | copy-start | bytes 3145732
  83.2 10.2 %all-to-all-start = ((f32[2,64,1,8192]{3,1,2,0:T(8,128)}), f32[2,64,1,8192]{3,1,2,0:T(8,128)}, u32[]{:S(2)}, u32[]{:S(2)}) async-start(f32[2,64,1,8192]{3,1,2,0:T(8,128)} %copy.37), calls=%async_computation | async-start | bytes 8388608 | tf_op jit(solution)/shard_map/all_to_all | solution.py:21
  94.1 10.7 %all-to-all-start.3 = ((f32[4,1,2048]{2,1,0:T(1,128)}), f32[4,1,2048]{2,1,0:T(1,128)S(1)}, u32[]{:S(2)}, u32[]{:S(2)}) async-start(f32[4,1,2048]{2,1,0:T(1,128)} %broadcast_in_dim.66), calls=%async_computation.3 | async-start | bytes 65536 | tf_op jit(solution)/shard_map/all_to_all | solution.py:35
  104.8 16.6 %copy-start.3 = (s32[2048]{0:T(1024)S(1)}, s32[2048]{0:T(1024)}, u32[]{:S(2)}) copy-start(s32[2048]{0:T(1024)} %param.10) | copy-start | bytes 24580
  104.8 69.1 %all-to-all-start.1 = ((f32[64,1,8192]{2,1,0:T(1,128)}), f32[64,1,8192]{2,1,0:T(1,128)S(1)}, u32[]{:S(2)}, u32[]{:S(2)}) async-start(f32[64,1,8192]{2,1,0:T(1,128)} %reduce_sum.87), calls=%async_computation.1 | async-start | bytes 4194304 | tf_op jit(solution)/shard_map/all_to_all | solution.py:29
  178.5 10.8 %all-to-all-start.2 = ((f32[4,1,1]{2,1,0:T(1,128)}), f32[4,1,1]{2,1,0:T(1,128)S(1)}, u32[]{:S(2)}, u32[]{:S(2)}) async-start(f32[4,1,1]{2,1,0:T(1,128)} %broadcast_in_dim.61), calls=%async_computation.2 | async-start | bytes 4096 | tf_op jit(solution)/shard_map/all_to_all | solution.py:35
where the time goes:
time: 191 us; the launch traced here: 190 us
  waiting for transfers between devices  59.5 us (31%)
  local copies, waits for them, and re-layouts  54.9 us (29%)
  starting transfers between devices  32.2 us (17%)
  other arithmetic  27.5 us (14%)
  matrix products  14.6 us (8%)
    all_to_all x1, waiting for transfers between devices, sum_in_two_steps(): lax.all_to_all(nearer, far, split_axis=0, concat_axis=0, tiled=True)  52 us
    while x32, local copies, waits for them, and re-layouts  25.9 us
    all_to_all x1, starting transfers between devices, sum_in_two_steps(): lax.all_to_all(nearer, far, split_axis=0, concat_axis=0, tiled=True)  16.5 us
    add x8, other arithmetic, step(): return (total + jnp.concatenate([sum_w, sum_g], axis=1), None)  11 us
    all_to_all x2, starting transfers between devices, copy_for_each(): return lax.all_to_all(copies, axis, split_axis=0, concat_axis=0, tiled=True)  9.94 us
    dynamic_slice x32, local copies, waits for them, and re-layouts, per_device(): lax.scan(step, empty, (codes_blocks, slot_blocks, weight_blocks, value_bl...  8.33 us
    dot_general x8, matrix products, step(): jnp.einsum('rn,rk->nk', scaled, spread, preferred_element_type=jnp.float32)  7.41 us
    dot_general x8, matrix products, step(): jnp.einsum('rn,rk->nk', pick, spread, preferred_element_type=jnp.float32)  7.19 us
  transfers between devices with their start and end apart: 4, of which 3 were waited for; matrix products, arithmetic and copies ran while one was open for 5% of the time, Pallas kernels for 0%

commit v1 on v0

v1 whole, which is shorter than its diff:
```python
import functools

import jax
import jax.numpy as jnp
from jax import lax
from jax.experimental import pallas as pl
from jax.experimental.pallas import tpu as pltpu
from jax.sharding import Mesh
from jax.sharding import PartitionSpec as P

BINS = 32
LAMBDA = 1.0
RING = 8
FEATS = 4
NODES = 128
ROWS = 2048
TILES = ROWS // 128
CHUNK = 8
CHUNKS = 8
WIDE = CHUNK * BINS
LONG = RING // 2
SHORT = RING // 2 - 1
LAG = 4
LAG2 = 4
MESH = pl.DeviceIdType.MESH
NT = (((1,), (1,)), ((), ()))


def iota(shape, dim):
    return lax.broadcasted_iota(jnp.int32, shape, dim)


def kernel(
    codes_ref, node_ref, bag_ref, resp_ref, slot_ref, feat_ref, bin_ref,
    gains_ref, best_ref, child_ref,
    turned, meta, flags, pick, spread_a, spread_b, hist, ring, part, arrived, gain_rows, gain_in,
    top, tops, node_of, bin_of,
    swap_send, swap_recv, flag_send, flag_recv, ring_send, ring_recv, far_send, far_recv,
    top_send, top_recv, gain_send, gain_recv,
):
    z, y, core, x = (lax.axis_index(name) for name in ("z", "y", "c", "x"))
    near = (1 - core) * z + core * y
    far = core * z + (1 - core) * y

    def along_near(place):
        return {"z": (1 - core) * place + core * z, "y": core * place + (1 - core) * y}

    def along_far(place):
        return {"z": core * place + (1 - core) * z, "y": (1 - core) * place + core * y}

    def wrap(place):
        return lax.rem(place + 2 * RING, RING)

    other = {"c": 1 - core}
    beside = [
        {"x": lax.rem(x + dx, FEATS), "c": lax.rem(core + dc, 2)}
        for dx in range(FEATS)
        for dc in range(2)
        if dx or dc
    ]

    barrier = pltpu.get_barrier_semaphore()
    greeted = [along_near(wrap(near + 1)), along_near(wrap(near - 1))]
    greeted += [along_far(wrap(far + step)) for step in range(1, RING)]
    greeted += beside
    for peer in greeted:
        pl.semaphore_signal(barrier, inc=1, device_id=peer, device_id_type=MESH)

    def remote(src, dst, send, recv, peer):
        return pltpu.make_async_remote_copy(
            src_ref=src, dst_ref=dst, send_sem=send, recv_sem=recv, device_id=peer, device_id_type=MESH
        )

    meta[0, 0] = node_ref[...].astype(jnp.float32)
    meta[0, 1] = bag_ref[...].astype(jnp.float32)
    meta[0, 2] = resp_ref[...].astype(jnp.float32)

    lane = iota((NODES, 128), 1)
    line = iota((NODES, 128), 0)
    feat_col = jnp.sum(jnp.where(lane == line, feat_ref[...], 0), axis=1, keepdims=True)
    bin_col = jnp.sum(jnp.where(lane == line, bin_ref[...], 0), axis=1, keepdims=True)
    same = jnp.where(lane == line, 1.0, 0.0).astype(jnp.bfloat16)
    split = jnp.where(lane == feat_col - x * 128, 1.0, 0.0).astype(jnp.bfloat16)
    bin_of[...] = jnp.broadcast_to(bin_col.astype(jnp.float32), (NODES, 128))
    both = jnp.concatenate([same, split], axis=0)
    line_f = line.astype(jnp.float32)
    for turn in range(ROWS // 256):
        rows = pl.ds(turn * 256, 256)
        part_codes = codes_ref[rows, :].astype(jnp.float32).astype(jnp.bfloat16)
        out = lax.dot_general(both, part_codes, NT, preferred_element_type=jnp.float32)
        for half in range(2):
            for chunk in range(CHUNKS):
                at = half * 64 + chunk * CHUNK
                turned[half, chunk, :, rows] = out[at : at + CHUNK]
        for sub in range(2):
            tile = turn * 2 + sub
            code = out[NODES:, sub * 128 : (sub + 1) * 128]
            mine = (line_f == meta[0, 0, tile : tile + 1, :]) & (code > bin_of[...])
            flags[x, tile : tile + 1, :] = jnp.sum(jnp.where(mine, 1.0, 0.0), axis=0, keepdims=True)

    pl.semaphore_wait(barrier, len(greeted))

    swap = [
        remote(turned.at[1 - core], turned.at[2], swap_send.at[0], swap_recv.at[0], other),
        remote(meta.at[0], meta.at[1], swap_send.at[1], swap_recv.at[1], other),
    ]
    for copy in swap:
        copy.start()
    flag_copies = [
        remote(
            flags.at[x], flags.at[x], flag_send.at[dx - 1], flag_recv.at[dx - 1], {"x": lax.rem(x + dx, FEATS)}
        )
        for dx in range(1, FEATS)
    ]
    for copy in flag_copies:
        copy.start()

    lane = iota((2 * NODES, 128), 1)
    line = iota((2 * NODES, 128), 0)
    near_size = (1 - core) * 16 + core * 2
    far_size = (1 - core) * 2 + core * 16
    wanted = (line // 32) * near_size + (lax.rem(line, 32) // 4) * far_size + lax.rem(line, 2)
    node_col = jnp.sum(jnp.where(slot_ref[...] == wanted, lane, 0), axis=1, keepdims=True)
    node_of[...] = jnp.broadcast_to(node_col.astype(jnp.float32), (2 * NODES, 128))
    weigh = lax.rem(iota((8, 128), 0), 4) < 2

    def fill_pick(source):
        for tile in range(TILES):
            node = meta[source, 0, tile : tile + 1, :]
            value = jnp.where(weigh, 1.0, meta[source, 2, tile : tile + 1, :])
            value = jnp.concatenate([value] * (2 * NODES // 8), axis=0)
            block = jnp.where(node_of[...] == node, value, 0.0).astype(jnp.bfloat16)
            pick[:, source * ROWS + tile * 128 : source * ROWS + (tile + 1) * 128] = block

    bins = iota((BINS, 128), 0).astype(jnp.bfloat16)

    def fill_spread(spread, chunk):
        for source in range(2):
            where = core if source == 0 else 2
            for tile in range(TILES):
                at = slice(tile * 128, (tile + 1) * 128)
                weight = jnp.broadcast_to(meta[source, 1, tile : tile + 1, :], (BINS, 128)).astype(jnp.bfloat16)
                for feature in range(CHUNK):
                    code = jnp.broadcast_to(turned[where, chunk, feature : feature + 1, at], (BINS, 128))
                    code = code.astype(jnp.bfloat16)
                    spread[
                        feature * BINS : (feature + 1) * BINS, source * ROWS + tile * 128 : source * ROWS + (tile + 1) * 128
                    ] = jnp.where(code <= bins, weight, jnp.zeros_like(weight))

    fill_pick(0)
    for copy in swap:
        copy.wait_recv()
    fill_pick(1)
    fill_spread(spread_a, 0)

    def ring_copy(chunk, step, is_long):
        way = 1 - 2 * lax.rem(chunk, 2)
        if not is_long:
            way = -way
        at = step - 1 + (0 if is_long else LONG)
        length = LONG if is_long else SHORT
        owner = wrap(near + way * (length + 1 - step))
        if step == 1:
            src = hist.at[chunk, pl.ds(pl.multiple_of(owner * 32, 32), 32), :]
        else:
            src = ring.at[chunk, at - 1]
        peer = along_near(wrap(near + way))
        return remote(src, ring.at[chunk, at], ring_send.at[chunk, at], ring_recv.at[chunk, at], peer), owner

    def ring_step(chunk, step, is_long):
        copy, owner = ring_copy(chunk, step, is_long)
        if step > 1:
            ring_copy(chunk, step - 1, is_long)[0].wait_recv()
            at = step - 2 + (0 if is_long else LONG)
            ring[chunk, at] = ring[chunk, at] + hist[chunk, pl.ds(pl.multiple_of(owner * 32, 32), 32), :]
        copy.start()

    def far_copy(chunk, step):
        place = wrap(far + step)
        return remote(
            part.at[chunk, place], arrived.at[chunk, far], far_send.at[chunk, step - 1], far_recv.at[chunk, step - 1],
            along_far(place),
        )

    def ring_end(chunk):
        ring_copy(chunk, LONG, True)[0].wait_recv()
        ring_copy(chunk, SHORT, False)[0].wait_recv()
        mine = hist[chunk, pl.ds(pl.multiple_of(near * 32, 32), 32), :]
        mine = mine + ring[chunk, LONG - 1] + ring[chunk, LONG + SHORT - 1]
        for place in range(RING):
            part[chunk, place] = mine[place * 4 : place * 4 + 4]
        arrived[chunk, far] = part[chunk, far]
        for step in range(1, RING):
            far_copy(chunk, step).start()

    last = lax.rem(iota((2, WIDE), 1), BINS) == BINS - 1

    def spread_last(row):
        row = jnp.where(last, row, 0.0)
        for shift in (1, 2, 4, 8, 16):
            row = row + pltpu.roll(row, WIDE - shift, 1)
        return row

    def chunk_gains(chunk):
        for step in range(1, RING):
            far_copy(chunk, step).wait_recv()
        mine = arrived[chunk, 0]
        for place in range(1, RING):
            mine = mine + arrived[chunk, place]
        left_w, left_g = mine[0:2], mine[2:4]
        total_w, total_g = spread_last(left_w), spread_last(left_g)
        right_w, right_g = total_w - left_w, total_g - left_g
        gains = (
            left_g * left_g / (left_w + LAMBDA)
            + right_g * right_g / (right_w + LAMBDA)
            - total_g * total_g / (total_w + LAMBDA)
        )
        at = pl.ds(pl.multiple_of(chunk * WIDE, WIDE), WIDE)
        gain_rows[0, :, at] = gains[0:1]
        gain_rows[1, :, at] = gains[1:2]

    def compute(chunk, spread, following):
        @pl.when(chunk < CHUNKS)
        def _():
            hist[chunk] = lax.dot_general(pick[...], spread[...], NT, preferred_element_type=jnp.float32)
            fill_spread(following, lax.rem(chunk + 1, CHUNKS))

    def moves(slot):
        def stage(lag, work):
            chunk = slot - lag

            @pl.when((chunk >= 0) & (chunk < CHUNKS))
            def _():
                work(chunk)

        for step in range(1, LONG + 1):
            def work(chunk, step=step):
                ring_step(chunk, step, True)
                if step <= SHORT:
                    ring_step(chunk, step, False)
            stage(LAG * (step - 1), work)
        stage(LAG * LONG, ring_end)
        stage(LAG * LONG + LAG2, chunk_gains)

    slots = CHUNKS + LAG * LONG + LAG2

    def pair(index, carry):
        compute(2 * index, spread_a, spread_b)
        moves(2 * index)
        compute(2 * index + 1, spread_b, spread_a)
        moves(2 * index + 1)
        return carry

    lax.fori_loop(0, (slots + 1) // 2, pair, 0)

    for node in range(2):
        largest = jnp.max(gain_rows[node], axis=1, keepdims=True)
        top[node] = jnp.broadcast_to(largest, (1, 128))
    tops[x * 2 + core] = top[core]
    top_copies = [
        remote(top.at[peer["c"]], tops.at[x * 2 + core], top_send.at[index], top_recv.at[index], peer)
        for index, peer in enumerate(beside)
    ]
    gain_copy = remote(gain_rows.at[1 - core], gain_in, gain_send, gain_recv, other)
    for copy in top_copies:
        copy.start()
    gain_copy.start()

    for copy in flag_copies:
        copy.wait_recv()
    right = flags[0] + flags[1] + flags[2] + flags[3]
    child_ref[...] = 2 * node_ref[...] + jnp.where(right > 0.5, 1, 0)

    for copy in swap + flag_copies:
        copy.wait_send()

    def drain(chunk, carry):
        for step in range(1, LONG + 1):
            ring_copy(chunk, step, True)[0].wait_send()
        for step in range(1, SHORT + 1):
            ring_copy(chunk, step, False)[0].wait_send()
        for step in range(1, RING):
            far_copy(chunk, step).wait_send()
        return carry

    lax.fori_loop(0, CHUNKS, drain, 0)

    gain_copy.wait_recv()
    own, got = gain_rows[core], gain_in[...]
    half = CHUNKS * WIDE
    gains_ref[:, :half] = jnp.where(core == 0, own, got)
    gains_ref[:, half:] = jnp.where(core == 0, got, own)
    for copy in top_copies:
        copy.wait_recv()
    best = tops[0]
    for place in range(1, 2 * FEATS):
        best = jnp.maximum(best, tops[place])
    best_ref[...] = best[:, :1]
    for copy in top_copies + [gain_copy]:
        copy.wait_send()


def per_device(codes, node_ids, bag, response, owner_slot, chosen_feature, chosen_bin):
    vmem = pl.BlockSpec(memory_space=pltpu.VMEM)
    f32 = jnp.float32
    dma = pltpu.SemaphoreType.DMA
    gains, best, child = pl.pallas_call(
        kernel,
        out_shape=(
            jax.ShapeDtypeStruct((1, 128 * BINS), f32),
            jax.ShapeDtypeStruct((1, 1), f32),
            jax.ShapeDtypeStruct((TILES, 128), jnp.int32),
        ),
        in_specs=[vmem] * 7,
        out_specs=(vmem, vmem, vmem),
        scratch_shapes=[
            pltpu.VMEM((3, CHUNKS, CHUNK, ROWS), f32),
            pltpu.VMEM((2, 3, TILES, 128), f32),
            pltpu.VMEM((FEATS, TILES, 128), f32),
            pltpu.VMEM((2 * NODES, 2 * ROWS), jnp.bfloat16),
            pltpu.VMEM((WIDE, 2 * ROWS), jnp.bfloat16),
            pltpu.VMEM((WIDE, 2 * ROWS), jnp.bfloat16),
            pltpu.VMEM((CHUNKS, 2 * NODES, WIDE), f32),
            pltpu.VMEM((CHUNKS, LONG + SHORT, 32, WIDE), f32),
            pltpu.VMEM((CHUNKS, RING, 4, WIDE), f32),
            pltpu.VMEM((CHUNKS, RING, 4, WIDE), f32),
            pltpu.VMEM((2, 1, CHUNKS * WIDE), f32),
            pltpu.VMEM((1, CHUNKS * WIDE), f32),
            pltpu.VMEM((2, 1, 128), f32),
            pltpu.VMEM((2 * FEATS, 1, 128), f32),
            pltpu.VMEM((2 * NODES, 128), f32),
            pltpu.VMEM((NODES, 128), f32),
            dma((2,)), dma((2,)),
            dma((FEATS - 1,)), dma((FEATS - 1,)),
            dma((CHUNKS, LONG + SHORT)), dma((CHUNKS, LONG + SHORT)),
            dma((CHUNKS, RING - 1)), dma((CHUNKS, RING - 1)),
            dma((2 * FEATS - 1,)), dma((2 * FEATS - 1,)),
            dma, dma,
        ],
        compiler_params=pltpu.CompilerParams(collective_id=0, has_side_effects=True),
        name="level_step",
    )(
        codes,
        node_ids.reshape(TILES, 128),
        bag.reshape(TILES, 128),
        response.reshape(TILES, 128),
        owner_slot.reshape(1, NODES),
        chosen_feature.reshape(1, NODES),
        chosen_bin.reshape(1, NODES),
    )
    return gains, best.reshape(1), child.reshape(ROWS)


def solution(mesh):
    split = Mesh(mesh.devices.reshape(RING, RING, 2, FEATS), ("z", "y", "c", "x"))
    rows = ("z", "y", "c")
    placed = (P(rows, "x"), P(rows), P(rows), P(rows), P(), P(), P())
    return jax.shard_map(
        per_device,
        mesh=split,
        in_specs=placed,
        out_specs=(P(rows, "x"), P(rows), P(rows)),
        check_vma=False,
    )
```

time: 191 us -> 59.1 us (0.31)
  the two profiles are of different devices: /device:TPU:24 before, /device:TPU:1 now
where the time goes in v1:
time: 59.1 us; the launch traced here: 58.9 us
  Pallas kernels  54.6 us (92%)
  between operations  2.4 us (4%)
  local copies, waits for them, and re-layouts  1.93 us (3%)
    pallas_call x1, Pallas kernels, per_device(): pl.pallas_call(kernel, out_shape=(jax.ShapeDtypeStruct((1, 128 * BINS), f...  54.6 us
    unnamed x4, local copies, waits for them, and re-layouts  1.93 us

profile of v1, /device:TPU:1, one launch (start us, length us, event | category | flops | bytes accessed | tf_op | source)
XLA Modules:
  0.0 58.9 jit_solution(2315934598753036302)
XLA Ops:
  0.6 54.6 %level_step.1 = (f32[1,4096]{1,0:T(1,128)}, f32[1,1]{1,0:T(1,128)}, s32[16,128]{1,0:T(8,128)}) custom-call(s32[2048,128]{1,0:T(8,128)} %codes_ref.1, s32[16,128]{1,0:T(8,128)} %bitcast.8, s32[16,128]{1,0:T(8,128)} %bitcast.9, bf16[16,128]{1,0:T(8,128)(2,1)} %bitcast.11, s32[1,128]{1,0:T(1,128)} %bitcast.12, s32[1,128]{1,0:T(1,128)} %bitcast.13, ...), custom_call_target="tpu_custom_call" | custom-call | tf_op jit(solution)/shard_map/level_step/pallas_call | solution.py:307
  55.2 0.0 copy-start
  55.2 1.3 %copy.13 = f32[1,4096]{1,0:T(1,128)} copy(f32[1,4096]{1,0:T(1,128)} %get-tuple-element.12) | data formatting | bytes 32768
  57.1 0.0 copy-done
  57.2 0.6 %copy.15 = s32[2048]{0:T(1024)} copy(s32[2048]{0:T(1024)S(1)} %bitcast.10) | data formatting | bytes 16384
Async XLA Ops:
  55.2 2.0 %copy-start = (s32[16,128]{1,0:T(8,128)S(1)}, s32[16,128]{1,0:T(8,128)}, u32[]{:S(2)}) copy-start(s32[16,128]{1,0:T(8,128)} %get-tuple-element.8) | copy-start | bytes 24580
